TPU v7x, 32 devices: a whole 2x2x4 slice. The times are simulated.
32 devices in a mesh: tgt: 8 (over y, x, core), src: 4 (over z).
Axes of the slice: x: 2, y: 2, z: 4, core: 2. Of those that a mesh axis runs over, the one named last changes fastest.
Arguments:
- fibre_points: float32 [3, 64, 64], P(None, ('tgt', 'src')), may hold values from -6 to 6
- shell_points: float32 [3, 128, 64], P(None, 'tgt', 'src'), may hold values from -7 to 7, as said below
- bending: float32 [64, 64], replicated, may hold values from -0.12 to 0.12
- shell_inverse: bfloat16 [3, 128, 64, 3, 64, 128], P(None, 'tgt', None, None, 'src'), may hold values from -0.0390625 to 0.0390625
Outputs:
- fibre_velocity: float32 [3, 64, 64], P(None, ('tgt', 'src'))
- shell_density: float32 [3, 128, 64], P(None, 'tgt', 'src')
Inputs may be any that keep to these rules, and one draw needn't show every extreme that they name: `shell_points`: every shell node lies on the sphere of radius 7 about the anchor.
All inputs are finite; a program needn't handle non-finite values.
Results may differ from a plain program's by a relative error of at most 0.0029.
Values may be sent and summed in bfloat16 or wider, within the bound.
A program may use at most 64 MiB of HBM per device.

v0:
```python
import math
import jax
import jax.numpy as jnp
from jax import lax
from jax.sharding import PartitionSpec as P

mobility = 1.0 / (8.0 * math.pi)
soften_sq = 0.0025


def stokes_flow(targets, sources, strength):
    delta_x = targets[0][:, None] - sources[0][None, :]
    delta_y = targets[1][:, None] - sources[1][None, :]
    delta_z = targets[2][:, None] - sources[2][None, :]
    dist_sq = delta_x * delta_x + delta_y * delta_y + delta_z * delta_z
    inv_root = lax.rsqrt(dist_sq + soften_sq)
    inv_cubed = inv_root * inv_root * inv_root
    projection = (
        delta_x * strength[0][None, :]
        + delta_y * strength[1][None, :]
        + delta_z * strength[2][None, :]
    ) * inv_cubed
    diagonal_part = (dist_sq + 2.0 * soften_sq) * inv_cubed
    flow_x = jnp.sum(diagonal_part * strength[0][None, :] + projection * delta_x, axis=1)
    flow_y = jnp.sum(diagonal_part * strength[1][None, :] + projection * delta_y, axis=1)
    flow_z = jnp.sum(diagonal_part * strength[2][None, :] + projection * delta_z, axis=1)
    return mobility * jnp.stack([flow_x, flow_y, flow_z])


def block_width(column_count, target_count):
    widest = 128
    while widest * 2 * target_count <= 1 << 20:
        widest = widest * 2
    return math.gcd(column_count, widest)


def source_sum(running, targets, places, pushes):
    block_size = block_width(places.shape[1], targets.shape[1])
    turns = places.shape[1] // block_size

    def add_block(counter, partial_value):
        offset = counter * block_size
        part_places = lax.dynamic_slice_in_dim(places, offset, block_size, 1)
        part_pushes = lax.dynamic_slice_in_dim(pushes, offset, block_size, 1)
        return partial_value + stokes_flow(targets, part_places, part_pushes)

    return lax.fori_loop(0, turns, add_block, running)


def fibre_fold(targets, running, pieces):
    return source_sum(running, targets, pieces[0].reshape(3, -1), pieces[1].reshape(3, -1))


def per_device(fibre_points, shell_points, bending, shell_inverse):
    shell_rows = lax.all_gather(shell_points, "src", axis=2, tiled=True)
    columns_pos = lax.all_gather(shell_points, "tgt", axis=1, tiled=True)
    forces = -jnp.einsum("cfm,nm->cfn", fibre_points, bending, precision=lax.Precision.HIGHEST)
    fibre_block = lax.all_gather(fibre_points, "src", axis=1, tiled=True)
    block_flat = fibre_block.reshape(3, -1)
    targets = jnp.concatenate([block_flat, shell_rows.reshape(3, -1)], axis=1)
    zeros_flow = jnp.zeros(targets.shape, jnp.float32)
    flow_all = fibre_fold(
        targets,
        zeros_flow,
        (
            lax.all_gather(fibre_points, "tgt", axis=1, tiled=True),
            lax.all_gather(forces, "tgt", axis=1, tiled=True),
        ),
    )
    block_count = block_flat.shape[1]
    fibre_part = flow_all[:, :block_count].reshape(fibre_block.shape)
    shell_part = flow_all[:, block_count:].reshape(shell_rows.shape)
    fibre_flow = lax.psum_scatter(fibre_part, "src", scatter_dimension=1, tiled=True)
    shell_flow = lax.psum_scatter(shell_part, "src", scatter_dimension=2, tiled=True)
    columns = lax.all_gather(shell_flow.astype(jnp.bfloat16), "tgt", axis=1, tiled=True)
    density_rows = -jnp.einsum(
        "xaqcbn,cnb->xaq", shell_inverse, columns, preferred_element_type=jnp.float32
    )
    density = lax.psum_scatter(density_rows, "src", scatter_dimension=2, tiled=True)
    column_density = lax.all_gather(density, "tgt", axis=1, tiled=True)
    zeros_back = jnp.zeros(block_flat.shape, jnp.float32)
    back_block = source_sum(
        zeros_back, block_flat, columns_pos.reshape(3, -1), column_density.reshape(3, -1)
    )
    shell_back = lax.psum_scatter(
        back_block.reshape(fibre_block.shape), "src", scatter_dimension=1, tiled=True
    )
    velocity = fibre_flow + shell_back
    return (velocity, density)


def solution(mesh):
    placed = (
        P(None, ("tgt", "src"), None),
        P(None, "tgt", "src"),
        P(),
        P(None, "tgt", None, None, "src", None),
    )
    return jax.shard_map(
        per_device,
        mesh=mesh,
        in_specs=placed,
        out_specs=(P(None, ("tgt", "src"), None), P(None, "tgt", "src")),
        check_vma=False,
    )
```

profile of v0, /device:TPU:0, one launch (start us, length us, event | category | flops | bytes accessed | tf_op | source)
XLA Modules:
  0.0 174.0 jit_solution(9149982009309895691)
XLA Ops:
  7.2 0.7 copy.22
  7.9 14.9 %all_gather.21 = f32[3,8,64]{2,0,1:T(4,128)S(1)} all-gather(f32[3,2,64]{2,0,1:T(4,128)S(1)} %copy.22), channel_id=1, replica_groups=mesh['tgt'=8,'src'=4] {'src'}, dimensions={1}, use_global_device_ids=true | all-gather | bytes 7680 | tf_op jit(solution)/shard_map/all_gather | solution.py:58
  22.8 9.1 %all_gather.23 = f32[3,16,64]{2,0,1:T(4,128)S(1)} all-gather(f32[3,2,64]{2,0,1:T(4,128)S(1)} %copy.22), channel_id=1, replica_groups=mesh['tgt'=8,'src'=4] {'tgt'}, dimensions={1}, use_global_device_ids=true | all-gather | bytes 13824 | tf_op jit(solution)/shard_map/all_gather | solution.py:66
  31.9 0.8 convolution_negate_fusion
  33.0 9.1 %all_gather.24 = f32[3,16,64]{2,0,1:T(4,128)S(1)} all-gather(f32[3,2,64]{2,0,1:T(4,128)S(1)} %convolution_negate_fusion), channel_id=1, replica_groups=mesh['tgt'=8,'src'=4] {'tgt'}, dimensions={1}, use_global_device_ids=true | all-gather | bytes 13824 | tf_op jit(solution)/shard_map/all_gather | solution.py:67
  42.1 0.8 copy.24
  42.9 13.3 %all_gather.22 = f32[3,16,64]{1,0,2:T(4,128)S(1)} all-gather(f32[3,16,16]{1,0,2:T(4,128)S(1)} %copy.24), channel_id=1, replica_groups=mesh['tgt'=8,'src'=4] {'src'}, dimensions={2}, use_global_device_ids=true | all-gather | bytes 15360 | tf_op jit(solution)/shard_map/all_gather | solution.py:55
  56.5 10.0 %while.9 = (s32[]{:T(128)}, f32[3,1536]{1,0:T(4,128)S(1)}, f32[3,1536]{1,0:T(4,128)S(1)}, f32[3,1024]{1,0:T(4,128)S(1)}, f32[3,1024]{1,0:T(4,128)S(1)}, /*index=...) while((s32[]{:T(128)}, f32[3,1536]{1,0:T(4,128)S(1)}, ...), condition=%wide.region_4.0_spmd.clone, body=%wide.region_0.0_spmd.clone.sunk | while | flops 24397832 | bytes 202961 | solution.py:47
  56.7 4.7 %fusion.45 = (f32[1536]{0:T(1024)S(1)}, f32[1536]{0:T(1024)S(1)}, f32[1536]{0:T(1024)S(1)}) fusion(f32[512]{0:T(512)S(1)} %bitcast.39, f32[512]{0:T(512)S(1)} %bitcast.42, f32[1536]{0:T(1024)S(1)} %get-tuple-element.215, f32[512]{0:T(512)S(1)} %bitcast.41, f32[1536]{0:T(1024)S(1)} %get-tuple-element.217, f32[512]{0:T(512)S(1)} %bitcast.43, ...), kind=kLoop, calls=%fused_computation.16.clone.1 | loop fusion | flops 24374784 | bytes 49152 | tf_op jit(solution)/shard_map/while/body/eval_jaxpr/reduce_sum | solution.py:24
  61.7 4.7 %fusion.45 = (f32[1536]{0:T(1024)S(1)}, f32[1536]{0:T(1024)S(1)}, f32[1536]{0:T(1024)S(1)}) fusion(f32[512]{0:T(512)S(1)} %bitcast.39, f32[512]{0:T(512)S(1)} %bitcast.42, f32[1536]{0:T(1024)S(1)} %get-tuple-element.215, f32[512]{0:T(512)S(1)} %bitcast.41, f32[1536]{0:T(1024)S(1)} %get-tuple-element.217, f32[512]{0:T(512)S(1)} %bitcast.43, ...), kind=kLoop, calls=%fused_computation.16.clone.1 | loop fusion | flops 24374784 | bytes 49152 | tf_op jit(solution)/shard_map/while/body/eval_jaxpr/reduce_sum | solution.py:24
  66.7 0.7 reshape.64
  67.5 8.3 %all_gather.25 = f32[3,128,16]{2,1,0:T(8,128)S(1)} all-gather(f32[3,16,16]{2,1,0:T(8,128)S(1)} %copy-done.1), channel_id=1, replica_groups=mesh['tgt'=8,'src'=4] {'tgt'}, dimensions={1}, use_global_device_ids=true | all-gather | bytes 27648 | tf_op jit(solution)/shard_map/all_gather | solution.py:56
  75.8 11.1 %reduce-scatter.8.cloned.1.call-done = f32[16,48]{1,0:T(8,128)} async-done(((f32[64,48]{1,0:T(8,128)}), f32[16,48]{1,0:T(8,128)}) %reduce-scatter.8.cloned.1.call-update) | async-done | bytes 3088
  86.9 0.8 reshape.65
  87.8 9.1 %all_gather.26 = bf16[3,128,16]{2,1,0:T(8,128)(2,1)S(1)} all-gather(bf16[3,16,16]{2,1,0:T(8,128)(2,1)S(1)} %copy.34), channel_id=1, replica_groups=mesh['tgt'=8,'src'=4] {'tgt'}, dimensions={1}, use_global_device_ids=true | all-gather | bytes 13824 | tf_op jit(solution)/shard_map/all_gather | solution.py:75
  97.1 19.8 %fusion.16 = f32[1,3,16,64,1,1]{3,0,5,4,2,1:T(1,128)S(1)} fusion(bf16[3,128,16,1,1,1]{1,3,0,2,5,4:T(2,128)(2,1)S(1)} %copy.30, bf16[3,16,64,3,16,128]{5,4,3,2,1,0:T(8,128)(2,1)} %param.9), kind=kOutput, calls=%fused_computation.32 | convolution fusion | flops 37748736 | bytes 37773312 | tf_op jit(solution)/shard_map/xaqcbn,cnb->xaq/dot_general | solution.py:76
  117.0 0.7 reshape.66
  118.3 0.6 dynamic-slice
  119.6 14.7 %reduce-scatter.10.cloned.1.call-done = f32[16,48]{1,0:T(8,128)} async-done(((f32[64,48]{1,0:T(8,128)}), f32[16,48]{1,0:T(8,128)}) %reduce-scatter.10.cloned.1.call-update) | async-done | bytes 3088
  134.3 0.8 reshape.67
  135.2 9.4 %all_gather.27 = f32[3,128,16]{2,1,0:T(8,128)S(1)} all-gather(f32[3,16,16]{2,1,0:T(8,128)S(1)} %copy.36), channel_id=1, replica_groups=mesh['tgt'=8,'src'=4] {'tgt'}, dimensions={1}, use_global_device_ids=true | all-gather | bytes 27648 | tf_op jit(solution)/shard_map/all_gather | solution.py:80
  144.8 5.6 %fusion.24 = (f32[512]{0:T(512)S(1)}, f32[512]{0:T(512)S(1)}, f32[512]{0:T(512)S(1)}) fusion(f32[2048]{0:T(1024)S(1)} %mul.302, f32[2048]{0:T(1024)S(1)} %sub.197, f32[512]{0:T(512)S(1)} %sub.195, f32[2048]{0:T(1024)S(1)} %sub.207, f32[512]{0:T(512)S(1)} %sub.205, f32[2048]{0:T(1024)S(1)} %sub.202, f32[512]{0:T(512)S(1)} %sub.200, f32[2048]{0:T(1024)S(1)} %mul.309, ...), kind=kLoop, calls=%fused_computation.50 | loop fusion | flops 32504320 | bytes 61440 | tf_op jit(solution)/shard_map/while/body/eval_jaxpr/reduce_sum | solution.py:24
  150.7 15.9 %all-reduce = f32[3,8,64]{2,1,0:T(8,128)S(1)} all-reduce(f32[3,8,64]{2,1,0:T(8,128)S(1)} %fusion.34), channel_id=5, replica_groups=mesh['tgt'=8,'src'=4] {'src'}, use_global_device_ids=true, to_apply=%region_5.0.clone | all-reduce | flops 1536 | bytes 12288
  166.6 0.6 constant_dynamic-slice_fusion.2
  (60 shorter events, 2.7 us)
Async XLA Ops:
  7.2 24.8 %copy-start = (f32[64,64]{1,0:T(8,128)S(1)}, f32[64,64]{1,0:T(8,128)}, u32[]{:S(2)}) copy-start(f32[64,64]{1,0:T(8,128)} %param.8) | copy-start | bytes 49156
  7.2 79.8 %reduce-scatter.8.cloned.1.call-start = ((), (), s32[]{:S(2)}) async-start(), calls=%async_computation.2 | async-start | bytes 40960
  56.5 11.0 %copy-start.1 = (f32[3,16,16]{2,1,0:T(8,128)S(1)}, f32[3,16,16]{2,1,0:T(8,128)}, u32[]{:S(2)}) copy-start(f32[3,16,16]{2,1,0:T(8,128)} %param.7) | copy-start | bytes 9220
  67.4 66.9 %reduce-scatter.10.cloned.1.call-start = ((), (), s32[]{:S(2)}) async-start(), calls=%async_computation.3 | async-start | bytes 40960
  97.1 21.3 %copy-start.3 = (u32[32]{0:T(128)S(1)}, u32[32]{0:T(128)}, u32[]{:S(2)}) copy-start(u32[32]{0:T(128)} %constant.79) | copy-start | bytes 388
  135.2 32.0 %copy-start.2 = (f32[3,16,16]{2,1,0:T(8,128)}, f32[3,16,16]{2,1,0:T(8,128)S(1)}, u32[]{:S(2)}) copy-start(f32[3,16,16]{2,1,0:T(8,128)S(1)} %copy.36) | copy-start | bytes 9220
Sparse Core Ops, SparseCore 0:
  67.5 19.3 reduce-scatter.7
  117.8 16.4 reduce-scatter.9
where the time goes:
time: 174 us
  blocking collectives  89.2 us (51%)
  waiting for transfers between devices  25.9 us (15%)
  matrix products  20.6 us (12%)
  other arithmetic  15.1 us (9%)
  between operations  14.8 us (9%)
  local copies, waits for them, and re-layouts  8.12 us (5%)
    unnamed x4, waiting for transfers between devices  25.9 us
    dot_general x1, matrix products, per_device(): jnp.einsum('xaqcbn,cnb->xaq', shell_inverse, columns, preferred_element_t...  19.8 us
    unnamed x1, blocking collectives  15.9 us
    reduce_sum x3, other arithmetic, stokes_flow(): jnp.sum(diagonal_part * strength[0][None, :] + projection * delta_x, axis=1)  15 us
    all_gather x1, blocking collectives, per_device(): fibre_block = lax.all_gather(fibre_points, 'src', axis=1, tiled=True)  14.9 us
    all_gather x1, blocking collectives, per_device(): shell_rows = lax.all_gather(shell_points, 'src', axis=2, tiled=True)  13.3 us
    all_gather x1, blocking collectives, per_device(): column_density = lax.all_gather(density, 'tgt', axis=1, tiled=True)  9.42 us
    all_gather x1, blocking collectives, per_device(): lax.all_gather(shell_flow.astype(jnp.bfloat16), 'tgt', axis=1, tiled=True)  9.14 us
  transfers between devices with their start and end apart: 2, of which 2 were waited for; matrix products, arithmetic and copies ran while one was open for 1% of the time, Pallas kernels for 0%

commit v1 on v0

--- a/solution.py
+++ b/solution.py
@@ -55,7 +55,12 @@
     shell_rows = lax.all_gather(shell_points, "src", axis=2, tiled=True)
     columns_pos = lax.all_gather(shell_points, "tgt", axis=1, tiled=True)
     forces = -jnp.einsum("cfm,nm->cfn", fibre_points, bending, precision=lax.Precision.HIGHEST)
-    fibre_block = lax.all_gather(fibre_points, "src", axis=1, tiled=True)
+    ring = [fibre_points]
+    for hop in range(3):
+        ring.append(lax.ppermute(ring[-1], "src", [(dev, (dev + 1) % 4) for dev in range(4)]))
+    fibre_block = jnp.roll(
+        jnp.concatenate(ring[::-1], axis=1), (lax.axis_index("src") + 1) * ring[0].shape[1], axis=1
+    )
     block_flat = fibre_block.reshape(3, -1)
     targets = jnp.concatenate([block_flat, shell_rows.reshape(3, -1)], axis=1)
     zeros_flow = jnp.zeros(targets.shape, jnp.float32)

time: 174 us -> 176 us (1.011)
  blocking collectives: 89.2 us -> 74.6 us
  waiting for transfers between devices: 25.9 us -> 36.7 us
  starting transfers between devices: 0.08 us -> 4.35 us
    all_gather x1 -> x0, blocking collectives: 14.9 us -> none  [per_device(): fibre_block = lax.all_gather(fibre_points, 'src', axis=1, tiled=True)]
    unnamed x4, waiting for transfers between devices: 25.9 us -> 32.6 us
    ppermute x0 -> x3, starting transfers between devices: none -> 4.28 us  [per_device(): lax.ppermute(ring[-1], 'src', [(dev, (dev + 1) % 4) for dev in range(4)])]
    ppermute x0 -> x3, waiting for transfers between devices: none -> 4.1 us  [per_device(): lax.ppermute(ring[-1], 'src', [(dev, (dev + 1) % 4) for dev in range(4)])]
    unnamed x20 -> x18, local copies, waits for them, and re-layouts: 6.08 us -> 6.09 us
  transfers between devices with their start and end apart: 2 -> 5, of which waited for: 2 -> 3; matrix products, arithmetic and copies ran while one was open for 1% -> 2% of each run, Pallas kernels for 0% -> 0%
where the time goes in v1:
time: 176 us
  blocking collectives  74.6 us (42%)
  waiting for transfers between devices  36.7 us (21%)
  matrix products  20.6 us (12%)
  other arithmetic  15.1 us (9%)
  between operations  14.8 us (8%)
  local copies, waits for them, and re-layouts  9.52 us (5%)
  starting transfers between devices  4.35 us (2%)
    unnamed x4, waiting for transfers between devices  32.6 us
    dot_general x1, matrix products, per_device(): jnp.einsum('xaqcbn,cnb->xaq', shell_inverse, columns, preferred_element_t...  19.8 us
    unnamed x1, blocking collectives  15.9 us
    reduce_sum x3, other arithmetic, stokes_flow(): jnp.sum(diagonal_part * strength[0][None, :] + projection * delta_x, axis=1)  15 us
    all_gather x1, blocking collectives, per_device(): shell_rows = lax.all_gather(shell_points, 'src', axis=2, tiled=True)  13.6 us
    all_gather x1, blocking collectives, per_device(): columns_pos = lax.all_gather(shell_points, 'tgt', axis=1, tiled=True)  9.47 us
    all_gather x1, blocking collectives, per_device(): column_density = lax.all_gather(density, 'tgt', axis=1, tiled=True)  9.41 us
    all_gather x1, blocking collectives, per_device(): lax.all_gather(shell_flow.astype(jnp.bfloat16), 'tgt', axis=1, tiled=True)  9.11 us
  transfers between devices with their start and end apart: 5, of which 3 were waited for; matrix products, arithmetic and copies ran while one was open for 2% of the time, Pallas kernels for 0%

profile of v1, /device:TPU:0, one launch (start us, length us, event | category | flops | bytes accessed | tf_op | source)
XLA Modules:
  0.0 175.8 jit_solution(12620558292414480773)
XLA Ops:
  7.2 3.1 %collective-permute-start = (f32[3,2,64]{2,1,0:T(2,128)}, f32[3,2,64]{2,1,0:T(2,128)S(1)}, u32[]{:S(2)}, u32[]{:S(2)}) collective-permute-start(f32[3,2,64]{2,1,0:T(2,128)} %param.6), channel_id=1, source_target_pairs={{0,1},{1,2},{2,3},{3,0},{4,5},{5,6},{6,7},{7,4},{8,9},{9,10},{10,1... | collective-permute-start | bytes 4616 | tf_op jit(solution)/shard_map/ppermute | solution.py:60
  10.3 0.7 copy.21
  11.0 0.8 copy.19
  11.9 9.5 %all_gather.21 = f32[3,128,16]{2,1,0:T(8,128)S(1)} all-gather(f32[3,16,16]{2,1,0:T(8,128)} %param.7), channel_id=1, replica_groups=mesh['tgt'=8,'src'=4] {'tgt'}, dimensions={1}, use_global_device_ids=true | all-gather | bytes 27648 | tf_op jit(solution)/shard_map/all_gather | solution.py:56
  21.3 0.8 convolution_negate_fusion
  22.2 13.6 %all_gather.18 = f32[3,16,64]{1,0,2:T(4,128)S(1)} all-gather(f32[3,16,16]{1,0,2:T(4,128)S(1)} %copy.19), channel_id=1, replica_groups=mesh['tgt'=8,'src'=4] {'src'}, dimensions={2}, use_global_device_ids=true | all-gather | bytes 15360 | tf_op jit(solution)/shard_map/all_gather | solution.py:55
  35.8 8.9 %all_gather.19 = f32[3,16,64]{2,0,1:T(4,128)S(1)} all-gather(f32[3,2,64]{2,0,1:T(4,128)S(1)} %copy.21), channel_id=1, replica_groups=mesh['tgt'=8,'src'=4] {'tgt'}, dimensions={1}, use_global_device_ids=true | all-gather | bytes 13824 | tf_op jit(solution)/shard_map/all_gather | solution.py:71
  44.9 8.3 %all_gather.20 = f32[3,16,64]{2,0,1:T(4,128)S(1)} all-gather(f32[3,2,64]{2,0,1:T(4,128)S(1)} %convolution_negate_fusion), channel_id=1, replica_groups=mesh['tgt'=8,'src'=4] {'tgt'}, dimensions={1}, use_global_device_ids=true | all-gather | bytes 13824 | tf_op jit(solution)/shard_map/all_gather | solution.py:72
  53.2 0.9 collective-permute-start.2
  54.5 4.1 %collective-permute-done.2 = f32[3,2,64]{2,1,0:T(2,128)S(1)} collective-permute-done((f32[3,2,64]{2,1,0:T(2,128)S(1)}, f32[3,2,64]{2,1,0:T(2,128)S(1)}, u32[]{:S(2)}, u32[]{:S(2)}) %collective-permute-start.2) | collective-permute-done | bytes 1568 | tf_op jit(solution)/shard_map/ppermute | solution.py:60
  58.6 1.4 concatenate.10
  60.1 10.0 %while.9 = (s32[]{:T(128)}, f32[3,1536]{1,0:T(4,128)S(1)}, f32[3,1536]{1,0:T(4,128)S(1)}, f32[3,1024]{1,0:T(4,128)S(1)}, f32[3,1024]{1,0:T(4,128)S(1)}, /*index=...) while((s32[]{:T(128)}, f32[3,1536]{1,0:T(4,128)S(1)}, ...), condition=%wide.region_4.5_spmd.clone, body=%wide.region_0.4_spmd.clone.sunk | while | flops 24397832 | bytes 202961 | solution.py:47
  60.3 4.7 %fusion.45 = (f32[1536]{0:T(1024)S(1)}, f32[1536]{0:T(1024)S(1)}, f32[1536]{0:T(1024)S(1)}) fusion(f32[512]{0:T(512)S(1)} %bitcast.39, f32[512]{0:T(512)S(1)} %bitcast.42, f32[1536]{0:T(1024)S(1)} %get-tuple-element.215, f32[512]{0:T(512)S(1)} %bitcast.41, f32[1536]{0:T(1024)S(1)} %get-tuple-element.217, f32[512]{0:T(512)S(1)} %bitcast.43, ...), kind=kLoop, calls=%fused_computation.16.clone.1 | loop fusion | flops 24374784 | bytes 49152 | tf_op jit(solution)/shard_map/while/body/eval_jaxpr/reduce_sum | solution.py:24
  65.3 4.7 %fusion.45 = (f32[1536]{0:T(1024)S(1)}, f32[1536]{0:T(1024)S(1)}, f32[1536]{0:T(1024)S(1)}) fusion(f32[512]{0:T(512)S(1)} %bitcast.39, f32[512]{0:T(512)S(1)} %bitcast.42, f32[1536]{0:T(1024)S(1)} %get-tuple-element.215, f32[512]{0:T(512)S(1)} %bitcast.41, f32[1536]{0:T(1024)S(1)} %get-tuple-element.217, f32[512]{0:T(512)S(1)} %bitcast.43, ...), kind=kLoop, calls=%fused_computation.16.clone.1 | loop fusion | flops 24374784 | bytes 49152 | tf_op jit(solution)/shard_map/while/body/eval_jaxpr/reduce_sum | solution.py:24
  70.3 0.7 reshape.64
  72.6 16.3 %reduce-scatter.8.cloned.1.call-done = f32[16,48]{1,0:T(8,128)} async-done(((f32[64,48]{1,0:T(8,128)}), f32[16,48]{1,0:T(8,128)}) %reduce-scatter.8.cloned.1.call-update) | async-done | bytes 3088
  88.9 0.8 reshape.65
  89.8 9.1 %all_gather.22 = bf16[3,128,16]{2,1,0:T(8,128)(2,1)S(1)} all-gather(bf16[3,16,16]{2,1,0:T(8,128)(2,1)S(1)} %copy.29), channel_id=1, replica_groups=mesh['tgt'=8,'src'=4] {'tgt'}, dimensions={1}, use_global_device_ids=true | all-gather | bytes 13824 | tf_op jit(solution)/shard_map/all_gather | solution.py:80
  99.0 19.8 %fusion.16 = f32[1,3,16,64,1,1]{3,0,5,4,2,1:T(1,128)S(1)} fusion(bf16[3,128,16,1,1,1]{1,3,0,2,5,4:T(2,128)(2,1)S(1)} %copy.25, bf16[3,16,64,3,16,128]{5,4,3,2,1,0:T(8,128)(2,1)} %param.9), kind=kOutput, calls=%fused_computation.32 | convolution fusion | flops 37748736 | bytes 37773312 | tf_op jit(solution)/shard_map/xaqcbn,cnb->xaq/dot_general | solution.py:81
  119.9 16.3 %reduce-scatter.10.cloned.1.call-done = f32[16,48]{1,0:T(8,128)} async-done(((f32[64,48]{1,0:T(8,128)}), f32[16,48]{1,0:T(8,128)}) %reduce-scatter.10.cloned.1.call-update) | async-done | bytes 3088
  136.2 0.8 reshape.67
  137.1 9.4 %all_gather.23 = f32[3,128,16]{2,1,0:T(8,128)S(1)} all-gather(f32[3,16,16]{2,1,0:T(8,128)S(1)} %copy.31), channel_id=1, replica_groups=mesh['tgt'=8,'src'=4] {'tgt'}, dimensions={1}, use_global_device_ids=true | all-gather | bytes 27648 | tf_op jit(solution)/shard_map/all_gather | solution.py:85
  146.8 5.5 %fusion.24 = (f32[512]{0:T(512)S(1)}, f32[512]{0:T(512)S(1)}, f32[512]{0:T(512)S(1)}) fusion(f32[2048]{0:T(1024)S(1)} %mul.306, f32[2048]{0:T(1024)S(1)} %sub.202, f32[512]{0:T(512)S(1)} %sub.200, f32[2048]{0:T(1024)S(1)} %sub.212, f32[512]{0:T(512)S(1)} %sub.210, f32[2048]{0:T(1024)S(1)} %sub.207, f32[512]{0:T(512)S(1)} %sub.205, f32[2048]{0:T(1024)S(1)} %mul.313, ...), kind=kLoop, calls=%fused_computation.50 | loop fusion | flops 32504320 | bytes 61440 | tf_op jit(solution)/shard_map/while/body/eval_jaxpr/reduce_sum | solution.py:24
  152.5 15.9 %all-reduce = f32[3,8,64]{2,1,0:T(8,128)S(1)} all-reduce(f32[3,8,64]{2,1,0:T(8,128)S(1)} %fusion.34), channel_id=5, replica_groups=mesh['tgt'=8,'src'=4] {'src'}, use_global_device_ids=true, to_apply=%region_5.6.clone | all-reduce | flops 1536 | bytes 12288
  (64 shorter events, 4.8 us)
Async XLA Ops:
  7.2 14.2 %copy-start = (f32[64,64]{1,0:T(8,128)S(1)}, f32[64,64]{1,0:T(8,128)}, u32[]{:S(2)}) copy-start(f32[64,64]{1,0:T(8,128)} %param.8) | copy-start | bytes 49156
  7.2 81.7 %reduce-scatter.8.cloned.1.call-start = ((), (), s32[]{:S(2)}) async-start(), calls=%async_computation.2 | async-start | bytes 40960
  7.2 37.4 %collective-permute-start = (f32[3,2,64]{2,1,0:T(2,128)}, f32[3,2,64]{2,1,0:T(2,128)S(1)}, u32[]{:S(2)}, u32[]{:S(2)}) collective-permute-start(f32[3,2,64]{2,1,0:T(2,128)} %param.6), channel_id=1, source_target_pairs={{0,1},{1,2},{2,3},{3,0},{4,5},{5,6},{6,7},{7,4},{8,9},{9,10},{10,1... | collective-permute-start | bytes 4616 | tf_op jit(solution)/shard_map/ppermute | solution.py:60
  44.6 8.5 %collective-permute-start.1 = (f32[3,2,64]{2,1,0:T(2,128)S(1)}, f32[3,2,64]{2,1,0:T(2,128)S(1)}, u32[]{:S(2)}, u32[]{:S(2)}) collective-permute-start(f32[3,2,64]{2,1,0:T(2,128)S(1)} %collective-permute-done), channel_id=1, source_target_pairs={{0,1},{1,2},{2,3},{3,0},{4,5},{5,6},{6,7},{7,4},{8,9},{9,10},{10,1... | collective-permute-start | bytes 4616 | tf_op jit(solution)/shard_map/ppermute | solution.py:60
  53.2 5.4 %collective-permute-start.2 = (f32[3,2,64]{2,1,0:T(2,128)S(1)}, f32[3,2,64]{2,1,0:T(2,128)S(1)}, u32[]{:S(2)}, u32[]{:S(2)}) collective-permute-start(f32[3,2,64]{2,1,0:T(2,128)S(1)} %collective-permute-done.1), channel_id=1, source_target_pairs={{0,1},{1,2},{2,3},{3,0},{4,5},{5,6},{6,7},{7,4},{8,9},{9,10},{10,1... | collective-permute-start | bytes 4616 | tf_op jit(solution)/shard_map/ppermute | solution.py:60
  60.1 11.3 %copy-start.2 = (u32[32]{0:T(128)S(1)}, u32[32]{0:T(128)}, u32[]{:S(2)}) copy-start(u32[32]{0:T(128)} %constant.108) | copy-start | bytes 388
  71.0 65.2 %reduce-scatter.10.cloned.1.call-start = ((), (), s32[]{:S(2)}) async-start(), calls=%async_computation.3 | async-start | bytes 40960
  137.1 31.9 %copy-start.1 = (f32[3,16,16]{2,1,0:T(8,128)}, f32[3,16,16]{2,1,0:T(8,128)S(1)}, u32[]{:S(2)}) copy-start(f32[3,16,16]{2,1,0:T(8,128)S(1)} %copy.31) | copy-start | bytes 9220
Sparse Core Ops, SparseCore 0:
  71.2 17.6 reduce-scatter.7
  119.7 16.4 reduce-scatter.9
